TPU v7x, 32 devices: a whole 2x2x4 slice. The times are simulated.
32 devices in a mesh: fsdp: 4 (over y, x), head: 4 (over z), tensor: 2 (over core).
Axes of the slice: x: 2, y: 2, z: 4, core: 2. Of those that a mesh axis runs over, the one named last changes fastest.
Arguments:
- activations: bfloat16 [2, 16, 197, 768], P(None, ('fsdp', 'head')), may hold values from -6 to 6
- w_qkv: bfloat16 [3, 768, 768], P(None, 'fsdp', 'head'), may hold values from -0.21875 to 0.21875
- w_out: bfloat16 [768, 768], P('head', 'fsdp'), may hold values from -0.875 to 0.875
- gain_one: float32 [768], replicated, may hold values from 0.5 to 1.5
- gain_two: float32 [768], replicated, may hold values from 0.5 to 1.5
- w_router: bfloat16 [768, 8], replicated, may hold values from -0.15625 to 0.15625
- w_in: bfloat16 [8, 768, 3072], P('head', 'fsdp', 'tensor'), may hold values from -0.21875 to 0.21875
- w_down: bfloat16 [8, 3072, 768], P('head', 'tensor', 'fsdp'), may hold values from -0.625 to 0.625
- routes: int32 [2, 16, 197, 2], P(None, ('fsdp', 'head')), may hold values from 0 to 7, as said below
- slot_index: int32 [2, 16, 197, 2], P(None, ('fsdp', 'head')), may hold values from 0 to 63, as said below
- keep_mask: int32 [2, 16, 197, 2], P(None, ('fsdp', 'head')), may hold values from 0 to 1, as said below
- cotangent: bfloat16 [2, 16, 197, 768], P(None, ('fsdp', 'head')), may hold values from -6 to 6
Outputs:
- block_out: bfloat16 [2, 16, 197, 768], P(None, ('fsdp', 'head'))
- grad_input: float32 [2, 16, 197, 768], P(None, ('fsdp', 'head'))
- grad_qkv: float32 [3, 768, 768], P(None, 'fsdp', 'head')
- grad_out: float32 [768, 768], P('head', 'fsdp')
- grad_gain_one: float32 [768], replicated
- grad_gain_two: float32 [768], replicated
- grad_router: float32 [768, 8], replicated
- grad_in: float32 [8, 768, 3072], P('head', 'fsdp', 'tensor')
- grad_down: float32 [8, 3072, 768], P('head', 'tensor', 'fsdp')
Inputs may be any that keep to these rules, and one draw needn't show every extreme that they name: `routes`: the 2 experts of a token differ. In every micro-batch and for every index of fsdp there is an expert that 72 or more rows of each device along head name. `slot_index`: among the kept pairs of one device's rows of one micro-batch that name one expert, slots are distinct. `keep_mask`: of one device's rows of one micro-batch, at most 64 pairs naming one expert are kept, and a pair is dropped only where 64 pairs of that expert are kept; in every micro-batch and index of fsdp some expert has exactly 64 kept pairs from each device along head.
All inputs are finite; a program needn't handle non-finite values.
Results may differ from a plain program's by a relative error of at most 0.02.
Values may be sent and summed in bfloat16 or wider, within the bound.
A program may use at most 192 MiB of HBM per device.

v0:
```python
import jax
import jax.numpy as jnp
from jax import lax
from jax.sharding import PartitionSpec as P

HD = 64
TOP = 2
CAP = 64


highest = lax.Precision.HIGHEST
norm_eps = 1e-06


def norm_rows(values, gain_vec):
    centre = values - jnp.mean(values, axis=-1, keepdims=True)
    spread = jnp.mean(centre * centre, axis=-1, keepdims=True)
    return centre * lax.rsqrt(spread + norm_eps) * gain_vec


def fetch_weights(w_qkv, w_out, w_in, w_down):
    return (
        lax.all_gather(w_qkv, "fsdp", axis=1, tiled=True),
        lax.all_gather(w_out, "fsdp", axis=1, tiled=True),
        lax.all_gather(w_in, "fsdp", axis=1, tiled=True),
        lax.all_gather(w_down, "fsdp", axis=2, tiled=True),
    )


def gelu_exact(values):
    return jax.nn.gelu(values, approximate=False)


def softmax_last(values):
    return jax.nn.softmax(values, axis=-1)


def on_device(
    activations,
    w_qkv,
    w_out,
    gain_one,
    gain_two,
    w_router,
    w_in,
    w_down,
    routes,
    slot_index,
    keep_mask,
    cotangent,
):
    f32 = jnp.float32
    bf16 = jnp.bfloat16
    micro_count, img_count, seq_length, model_width = activations.shape
    groups = lax.axis_size("head")
    local_heads = w_qkv.shape[2] // HD
    local_experts = w_in.shape[0]
    total_experts = local_experts * groups
    slot_count = total_experts * CAP
    tok_rows = img_count * seq_length
    head_scale = HD ** (-0.5)
    grad_qkv = jnp.zeros((3, model_width, w_qkv.shape[2]), f32)
    grad_out = jnp.zeros((w_out.shape[0], model_width), f32)
    grad_in = jnp.zeros((local_experts, model_width, w_in.shape[2]), f32)
    grad_down = jnp.zeros((local_experts, w_down.shape[1], model_width), f32)
    grad_gain_one = jnp.zeros((model_width,), f32)
    grad_gain_two = jnp.zeros((model_width,), f32)
    grad_router = jnp.zeros((model_width, total_experts), f32)
    slot_ids = jnp.arange(slot_count, dtype=jnp.int32)
    expert_ids = jnp.arange(total_experts, dtype=jnp.int32)
    router_full = w_router.astype(f32)
    outputs = []
    input_grads = []
    for micro_index in range(micro_count):
        qkv_full, out_full, in_full, down_full = fetch_weights(w_qkv, w_out, w_in, w_down)
        inputs = activations[micro_index].astype(f32)
        normed, norm_back_one = jax.vjp(norm_rows, inputs, gain_one)
        rows_all = lax.all_gather(normed.astype(bf16), "head", axis=0, tiled=True)
        image_total = rows_all.shape[0]
        head_shape = (image_total, seq_length, local_heads, HD)
        project = jnp.einsum("bsd,pde->pbse", rows_all, qkv_full, preferred_element_type=f32)
        queries = (project[0] * head_scale).astype(bf16).reshape(head_shape)
        key_rows = project[1].astype(bf16).reshape(head_shape)
        value_rows = project[2].astype(bf16).reshape(head_shape)
        scores = jnp.einsum("bqhd,bkhd->bhqk", queries, key_rows, preferred_element_type=f32)
        top_score = jnp.max(scores, axis=-1, keepdims=True)
        expo_scores = jnp.exp(scores - top_score)
        row_total = jnp.sum(expo_scores, axis=-1, keepdims=True)
        log_total = top_score + jnp.log(row_total)
        attn_probs = (expo_scores / row_total).astype(bf16)
        mixed_heads = jnp.einsum(
            "bhqk,bkhd->bqhd", attn_probs, value_rows, preferred_element_type=f32
        )
        mixed_heads = mixed_heads.reshape(image_total, seq_length, local_heads * HD).astype(bf16)
        partial_att = jnp.einsum("bsc,cd->bsd", mixed_heads, out_full, preferred_element_type=f32)
        attended = lax.psum_scatter(
            partial_att.astype(jnp.bfloat16), "head", scatter_dimension=0, tiled=True
        ).astype(jnp.float32)
        hidden = inputs + attended
        normed_two, norm_back_two = jax.vjp(norm_rows, hidden, gain_two)
        token_low = normed_two.astype(bf16).reshape(tok_rows, model_width)
        logits = jnp.dot(token_low, w_router, preferred_element_type=f32)
        gate_probs, softmax_back = jax.vjp(softmax_last, logits)
        route_rows = routes[micro_index].reshape(tok_rows, TOP)
        slot_rows = slot_index[micro_index].reshape(tok_rows, TOP)
        keep_int = keep_mask[micro_index].reshape(tok_rows, TOP)
        keep_rows = keep_int.astype(f32)
        chosen = (route_rows[:, :, None] == expert_ids[None, None, :]).astype(f32)
        gate_values = jnp.sum(gate_probs[:, None, :] * chosen, axis=2) * keep_rows
        flat_slot = route_rows * CAP + slot_rows
        onehot = (
            (flat_slot.T[:, :, None] == slot_ids[None, None, :]) & (keep_int.T[:, :, None] == 1)
        ).astype(bf16)
        buffer = jnp.einsum("ktc,td->cd", onehot, token_low, preferred_element_type=f32).astype(
            bf16
        )
        buffer = buffer.reshape(groups, local_experts, CAP, model_width)
        received = lax.all_to_all(buffer, "head", split_axis=0, concat_axis=0, tiled=True)
        up_proj = jnp.einsum("gecd,edf->gecf", received, in_full, preferred_element_type=f32)
        active = gelu_exact(up_proj).astype(bf16)
        partial_out = jnp.einsum("gecf,efd->gecd", active, down_full, preferred_element_type=f32)
        expert_out = (
            lax.psum(partial_out.astype(jnp.bfloat16), "tensor").astype(jnp.float32).astype(bf16)
        )
        returned = lax.all_to_all(
            expert_out, "head", split_axis=0, concat_axis=0, tiled=True
        ).reshape(slot_count, model_width)
        picked = jnp.einsum("ktc,cd->ktd", onehot, returned, preferred_element_type=f32)
        moe_out = jnp.sum(gate_values.T[:, :, None] * picked, axis=0)
        block_out = hidden + moe_out.reshape(img_count, seq_length, model_width)
        outputs.append(block_out.astype(bf16))
        upstream = cotangent[micro_index].astype(f32).reshape(tok_rows, model_width)
        gate_grad = jnp.einsum("td,ktd->tk", upstream, picked) * keep_rows
        weighted = (gate_values.T[:, :, None] * upstream[None, :, :]).astype(bf16)
        slot_grad = jnp.einsum("ktc,ktd->cd", onehot, weighted, preferred_element_type=f32).astype(
            bf16
        )
        slot_grad = lax.all_to_all(
            slot_grad.reshape(groups, local_experts, CAP, model_width),
            "head",
            split_axis=0,
            concat_axis=0,
            tiled=True,
        )
        grad_down = grad_down + jnp.einsum(
            "gecf,gecd->efd", active, slot_grad, preferred_element_type=f32
        )
        active_grad = jnp.einsum("gecd,efd->gecf", slot_grad, down_full, preferred_element_type=f32)
        gelu_back = jax.vjp(gelu_exact, up_proj)[1]
        up_grad = gelu_back(active_grad)[0].astype(bf16)
        grad_in = grad_in + jnp.einsum(
            "gecd,gecf->edf", received, up_grad, preferred_element_type=f32
        )
        partial_in = jnp.einsum("gecf,edf->gecd", up_grad, in_full, preferred_element_type=f32)
        slot_input = lax.psum(partial_in.astype(jnp.bfloat16), "tensor").astype(jnp.float32)
        slot_input = (
            lax.all_to_all(
                slot_input.astype(jnp.bfloat16), "head", split_axis=0, concat_axis=0, tiled=True
            )
            .astype(slot_input.dtype)
            .reshape(slot_count, model_width)
        )
        token_grad = jnp.sum(
            keep_rows[:, :, None] * jnp.take(slot_input, flat_slot, axis=0), axis=1
        )
        prob_grad = jnp.sum(gate_grad[:, :, None] * chosen, axis=1)
        logit_grad = softmax_back(prob_grad)[0]
        grad_router = grad_router + jnp.dot(token_low.astype(f32).T, logit_grad, precision=highest)
        token_grad = token_grad + jnp.dot(logit_grad, router_full.T, precision=highest)
        hidden_part, gain_part_two = norm_back_two(
            token_grad.reshape(img_count, seq_length, model_width)
        )
        grad_gain_two = grad_gain_two + gain_part_two
        hidden_grad = upstream.reshape(img_count, seq_length, model_width) + hidden_part
        att_grad_all = lax.all_gather(hidden_grad.astype(bf16), "head", axis=0, tiled=True)
        grad_out = grad_out + jnp.einsum(
            "bsc,bsd->cd", mixed_heads, att_grad_all, preferred_element_type=f32
        )
        mixed_grad = jnp.einsum("bsd,cd->bsc", att_grad_all, out_full, preferred_element_type=f32)
        mixed_grad = mixed_grad.astype(bf16).reshape(head_shape)
        scores_again = jnp.einsum("bqhd,bkhd->bhqk", queries, key_rows, preferred_element_type=f32)
        attn_full = jnp.exp(scores_again - log_total)
        attn_low = attn_full.astype(bf16)
        value_grad = jnp.einsum(
            "bhqk,bqhd->bkhd", attn_low, mixed_grad, preferred_element_type=f32
        ).astype(bf16)
        prob_grads = jnp.einsum(
            "bqhd,bkhd->bhqk", mixed_grad, value_rows, preferred_element_type=f32
        )
        row_delta = jnp.sum(prob_grads * attn_full, axis=-1, keepdims=True)
        score_grad = (attn_full * (prob_grads - row_delta)).astype(bf16)
        query_grad = (
            jnp.einsum("bhqk,bkhd->bqhd", score_grad, key_rows, preferred_element_type=f32)
            * head_scale
        ).astype(bf16)
        key_grad = jnp.einsum(
            "bhqk,bqhd->bkhd", score_grad, queries, preferred_element_type=f32
        ).astype(bf16)
        proj_grad = jnp.stack([query_grad, key_grad, value_grad]).reshape(
            3, image_total, seq_length, local_heads * HD
        )
        grad_qkv = grad_qkv + jnp.einsum(
            "bsd,pbse->pde", rows_all, proj_grad, preferred_element_type=f32
        )
        row_part = jnp.einsum("pbse,pde->bsd", proj_grad, qkv_full, preferred_element_type=f32)
        row_grad = lax.psum_scatter(
            row_part.astype(jnp.bfloat16), "head", scatter_dimension=0, tiled=True
        ).astype(jnp.float32)
        input_part, gain_part_one = norm_back_one(row_grad)
        grad_gain_one = grad_gain_one + gain_part_one
        input_grads.append(hidden_grad + input_part)
    grad_qkv, grad_out, grad_in, grad_down = (
        lax.psum_scatter(
            grad_qkv.astype(jnp.bfloat16), "fsdp", scatter_dimension=1, tiled=True
        ).astype(jnp.float32),
        lax.psum_scatter(
            grad_out.astype(jnp.bfloat16), "fsdp", scatter_dimension=1, tiled=True
        ).astype(jnp.float32),
        lax.psum_scatter(
            grad_in.astype(jnp.bfloat16), "fsdp", scatter_dimension=1, tiled=True
        ).astype(jnp.float32),
        lax.psum_scatter(
            grad_down.astype(jnp.bfloat16), "fsdp", scatter_dimension=2, tiled=True
        ).astype(jnp.float32),
    )
    grad_gain_one, grad_gain_two, grad_router = lax.psum(
        (grad_gain_one, grad_gain_two, grad_router), ("fsdp", "head")
    )
    return (
        jnp.stack(outputs),
        jnp.stack(input_grads),
        grad_qkv,
        grad_out,
        grad_gain_one,
        grad_gain_two,
        grad_router,
        grad_in,
        grad_down,
    )


def solution(mesh):
    in_specs = (
        P(None, ("fsdp", "head"), None, None),
        P(None, "fsdp", "head"),
        P("head", "fsdp"),
        P(),
        P(),
        P(),
        P("head", "fsdp", "tensor"),
        P("head", "tensor", "fsdp"),
        P(None, ("fsdp", "head"), None, None),
        P(None, ("fsdp", "head"), None, None),
        P(None, ("fsdp", "head"), None, None),
        P(None, ("fsdp", "head"), None, None),
    )
    out_specs = (
        P(None, ("fsdp", "head"), None, None),
        P(None, ("fsdp", "head"), None, None),
        P(None, "fsdp", "head"),
        P("head", "fsdp"),
        P(),
        P(),
        P(),
        P("head", "fsdp", "tensor"),
        P("head", "tensor", "fsdp"),
    )
    return jax.shard_map(
        on_device, mesh=mesh, in_specs=in_specs, out_specs=out_specs, check_vma=False
    )
```

profile of v0, /device:TPU:0, one launch (start us, length us, event | category | flops | bytes accessed | tf_op | source)
XLA Modules:
  0.0 772.3 jit_solution(16826512225389969451)
XLA Ops:
  13.7 11.0 %all_gather.30 = bf16[192,768]{0,1:T(8,128)(2,1)S(1)} all-gather(bf16[192,192]{0,1:T(8,128)(2,1)S(1)} %copy.166), channel_id=1, replica_groups=mesh['fsdp'=4,'head'=4,'tensor'=2] {'fsdp'}, dimensions={1}, use_global_device_ids=true | all-gather | bytes 368640 | tf_op jit(solution)/shard_map/all_gather | solution.py:24
  25.0 15.8 %all_gather.29 = bf16[3,768,192]{2,0,1:T(4,128)(2,1)S(1)} all-gather(bf16[3,192,192]{2,0,1:T(4,128)(2,1)S(1)} %copy.163), channel_id=1, replica_groups=mesh['fsdp'=4,'head'=4,'tensor'=2] {'fsdp'}, dimensions={1}, use_global_device_ids=true | all-gather | bytes 1105920 | tf_op jit(solution)/shard_map/all_gather | solution.py:23
  41.7 5.1 all-gather.7.cloned.1.call-done
  54.5 24.7 %all-gather.13.cloned.1.call-done = bf16[4,197,768]{2,1,0:T(8,128)(2,1)} async-done(((bf16[1,197,768]{2,1,0:T(8,128)(2,1)}), bf16[4,197,768]{2,1,0:T(8,128)(2,1)}) %all-gather.13.cloned.1.call-update) | async-done | bytes 1210384 | tf_op jit(solution)/shard_map/all_gather | solution.py:78
  88.5 23.1 %reduce-scatter.13.cloned.1.call-done = bf16[1,197,768]{2,1,0:T(8,128)(2,1)} async-done(((bf16[4,197,768]{2,1,0:T(8,128)(2,1)}), bf16[1,197,768]{2,1,0:T(8,128)(2,1)}) %reduce-scatter.13.cloned.1.call-update) | async-done | bytes 302608 | tf_op jit(solution)/shard_map/reduce_scatter | solution.py:96
  114.0 28.7 %reduce-scatter.15.cloned.1.call-done = bf16[1,197,768]{2,1,0:T(8,128)(2,1)} async-done(((bf16[4,197,768]{2,1,0:T(8,128)(2,1)}), bf16[1,197,768]{2,1,0:T(8,128)(2,1)}) %reduce-scatter.15.cloned.1.call-update) | async-done | bytes 302608 | tf_op jit(solution)/shard_map/reduce_scatter | solution.py:96
  152.5 18.6 %all-to-all-done = bf16[4,2,64,768]{3,2,1,0:T(8,128)(2,1)S(1)} async-done(((bf16[4,2,64,768]{3,2,1,0:T(8,128)(2,1)}), bf16[4,2,64,768]{3,2,1,0:T(8,128)(2,1)S(1)}, u32[]{:S(2)}, u32[]{:S(2)}) %all-to-all-start) | async-done | bytes 786464 | tf_op jit(solution)/shard_map/all_to_all | solution.py:118
  175.7 11.8 %fusion.35 = (bf16[4,2,64,1536]{3,2,0,1:T(8,128)(2,1)S(1)}, f32[4,2,64,1536]{3,2,0,1:T(8,128)}, f32[2,4,64,1536]{3,2,1,0:T(8,128)}) fusion(bf16[2,768,1536]{2,1,0:T(8,128)(2,1)} %all-gather.9.cloned.1.call-done, bf16[4,2,64,768]{3,2,1,0:T(8,128)(2,1)} %copy-done.52), kind=kOutput, calls=%fused_computation.49 | convolution fusion | flops 1259077632 | bytes 13369344 | tf_op jit(solution)/shard_map/gecd,edf->gecf/dot_general | solution.py:119
  187.5 7.6 all-to-all-done.2
  195.1 11.3 %fusion.27 = (bf16[4,2,64,1536]{3,2,0,1:T(8,128)(2,1)}, f32[4,2,64,1536]{3,2,0,1:T(8,128)}, f32[2,4,64,1536]{3,2,1,0:T(8,128)}) fusion(bf16[2,768,1536]{2,1,0:T(8,128)(2,1)} %all-gather.9.cloned.1.call-done, bf16[4,2,64,768]{3,2,1,0:T(8,128)(2,1)} %all-to-all-done.2), kind=kOutput, calls=%fused_computation.35 | convolution fusion | flops 1259077632 | bytes 13369344 | tf_op jit(solution)/shard_map/gecd,edf->gecf/dot_general | solution.py:119
  213.6 19.6 %all-reduce.8.cloned.1.call-done = (bf16[4,2,64,768]{3,2,0,1:T(8,128)(2,1)}, bf16[4,2,64,768]{3,2,0,1:T(8,128)(2,1)}) async-done(((bf16[4,2,64,768]{3,2,0,1:T(8,128)(2,1)}, bf16[4,2,64,768]{3,2,0,1:T(8,128)(2,1)}), (bf16[4,2,64,768]{3,2,0,1:T(8,128)(2,1)}, bf16[4,2,64,768]{3,2,0,1:T(8,128)(2,1)})) %all-reduce.8.cloned.1.call-update) | async-done | bytes 1572880 | tf_op jit(solution)/shard_map/psum | solution.py:123
  235.3 4.9 all-to-all-start.1
  244.3 16.4 %all-to-all-done.1 = bf16[4,2,64,768]{3,2,1,0:T(8,128)(2,1)S(1)} async-done(((bf16[4,2,64,768]{3,2,1,0:T(8,128)(2,1)}), bf16[4,2,64,768]{3,2,1,0:T(8,128)(2,1)S(1)}, u32[]{:S(2)}, u32[]{:S(2)}) %all-to-all-start.1) | async-done | bytes 786464 | tf_op jit(solution)/shard_map/all_to_all | solution.py:125
  267.6 17.5 %all-to-all-done.3 = bf16[4,2,64,768]{3,2,1,0:T(8,128)(2,1)} async-done(((bf16[4,2,64,768]{3,2,1,0:T(8,128)(2,1)}), bf16[4,2,64,768]{3,2,1,0:T(8,128)(2,1)}, u32[]{:S(2)}, u32[]{:S(2)}) %all-to-all-start.3) | async-done | bytes 786464 | tf_op jit(solution)/shard_map/all_to_all | solution.py:125
  302.2 16.9 %all-to-all-done.6 = bf16[4,2,64,768]{3,2,1,0:T(8,128)(2,1)} async-done(((bf16[4,2,64,768]{3,2,1,0:T(8,128)(2,1)}), bf16[4,2,64,768]{3,2,1,0:T(8,128)(2,1)}, u32[]{:S(2)}, u32[]{:S(2)}) %all-to-all-start.6) | async-done | bytes 786464 | tf_op jit(solution)/shard_map/all_to_all | solution.py:138
  323.4 6.4 fusion.33
  335.6 7.4 all-to-all-done.4
  343.1 6.4 fusion.41
  355.3 19.6 %all-reduce.6.cloned.1.call-done = (bf16[4,2,64,768]{3,2,0,1:T(8,128)(2,1)}, bf16[4,2,64,768]{3,2,0,1:T(8,128)(2,1)}) async-done(((bf16[4,2,64,768]{3,2,0,1:T(8,128)(2,1)}, bf16[4,2,64,768]{3,2,0,1:T(8,128)(2,1)}), (bf16[4,2,64,768]{3,2,0,1:T(8,128)(2,1)}, bf16[4,2,64,768]{3,2,0,1:T(8,128)(2,1)})) %all-reduce.6.cloned.1.call-update) | async-done | bytes 1572880 | tf_op jit(solution)/shard_map/psum | solution.py:155
  377.0 5.0 all-to-all-start.5
  392.0 10.6 %all-to-all-done.5 = bf16[4,2,64,768]{3,2,1,0:T(8,128)(2,1)} async-done(((bf16[4,2,64,768]{3,2,1,0:T(8,128)(2,1)}), bf16[4,2,64,768]{3,2,1,0:T(8,128)(2,1)}, u32[]{:S(2)}, u32[]{:S(2)}) %all-to-all-start.5) | async-done | bytes 786464 | tf_op jit(solution)/shard_map/all_to_all | solution.py:157
  416.9 9.7 %all-to-all-done.7 = bf16[4,2,64,768]{3,2,1,0:T(8,128)(2,1)} async-done(((bf16[4,2,64,768]{3,2,1,0:T(8,128)(2,1)}), bf16[4,2,64,768]{3,2,1,0:T(8,128)(2,1)}, u32[]{:S(2)}, u32[]{:S(2)}) %all-to-all-start.7) | async-done | bytes 786464 | tf_op jit(solution)/shard_map/all_to_all | solution.py:157
  432.6 6.6 fusion.116
  440.5 5.7 fusion.117
  454.3 27.1 %all-gather.17.cloned.1.call-done = bf16[4,197,768]{2,1,0:T(8,128)(2,1)} async-done(((bf16[1,197,768]{2,1,0:T(8,128)(2,1)}), bf16[4,197,768]{2,1,0:T(8,128)(2,1)}) %all-gather.17.cloned.1.call-update) | async-done | bytes 1210384 | tf_op jit(solution)/shard_map/all_gather | solution.py:175
  486.7 27.1 %all-gather.15.cloned.1.call-done = bf16[4,197,768]{2,1,0:T(8,128)(2,1)} async-done(((bf16[1,197,768]{2,1,0:T(8,128)(2,1)}), bf16[4,197,768]{2,1,0:T(8,128)(2,1)}) %all-gather.15.cloned.1.call-update) | async-done | bytes 1210384 | tf_op jit(solution)/shard_map/all_gather | solution.py:175
  544.5 4.9 fusion.1
  563.1 15.0 %reduce-scatter.25.cloned.1.call-done = bf16[192,576]{1,0:T(8,128)(2,1)} async-done(((bf16[768,576]{1,0:T(8,128)(2,1)}), bf16[192,576]{1,0:T(8,128)(2,1)}) %reduce-scatter.25.cloned.1.call-update) | async-done | bytes 221200
  580.6 30.2 %reduce-scatter.17.cloned.1.call-done = bf16[1,197,768]{2,1,0:T(8,128)(2,1)} async-done(((bf16[4,197,768]{2,1,0:T(8,128)(2,1)}), bf16[1,197,768]{2,1,0:T(8,128)(2,1)}) %reduce-scatter.17.cloned.1.call-update) | async-done | bytes 302608 | tf_op jit(solution)/shard_map/reduce_scatter | solution.py:206
  612.0 30.5 %reduce-scatter.19.cloned.1.call-done = bf16[1,197,768]{2,1,0:T(8,128)(2,1)} async-done(((bf16[4,197,768]{2,1,0:T(8,128)(2,1)}), bf16[1,197,768]{2,1,0:T(8,128)(2,1)}) %reduce-scatter.19.cloned.1.call-update) | async-done | bytes 302608 | tf_op jit(solution)/shard_map/reduce_scatter | solution.py:206
  648.8 76.4 %all-reduce = (f32[768]{0:T(1024)}, f32[768]{0:T(1024)}, f32[768,8]{0,1:T(8,128)}) all-reduce(f32[768]{0:T(1024)S(1)} %add.174, f32[768]{0:T(1024)S(1)} %add.175, f32[768,8]{0,1:T(8,128)S(1)} %convolution_add_fusion.2), channel_id=1, replica_groups=mesh['fsdp'=4,'head'=4,'tensor'=2] {'fsdp','head'}, use_global_device_ids=true, to_apply=%region_50.52 | all-reduce | flops 7680 | bytes 61440 | tf_op jit(solution)/shard_map/psum | solution.py:226
  728.1 33.3 %reduce-scatter.23.cloned.1.call-done = bf16[2,1536,192]{1,2,0:T(8,128)(2,1)} async-done(((bf16[2,1536,768]{1,2,0:T(8,128)(2,1)}), bf16[2,1536,192]{1,2,0:T(8,128)(2,1)}) %reduce-scatter.23.cloned.1.call-update) | async-done | bytes 1179664 | tf_op jit(solution)/shard_map/reduce_scatter | solution.py:222
  (481 shorter events, 198.8 us)
Async XLA Ops:
  8.0 234.8 %copy-start = (bf16[768,8]{0,1:T(8,128)(2,1)S(1)}, bf16[768,8]{0,1:T(8,128)(2,1)}, u32[]{:S(2)}) copy-start(bf16[768,8]{0,1:T(8,128)(2,1)} %param.19) | copy-start | bytes 36868
  8.0 38.7 %all-gather.7.cloned.1.call-start = ((), (), s32[]{:S(2)}) async-start(), calls=%async_computation.16 | async-start | bytes 1536000 | tf_op jit(solution)/shard_map/all_gather | solution.py:78
  12.8 66.5 %all-gather.13.cloned.1.call-start = ((), (), s32[]{:S(2)}) async-start(), calls=%async_computation.20 | async-start | bytes 1536000 | tf_op jit(solution)/shard_map/all_gather | solution.py:78
  13.6 98.0 %reduce-scatter.13.cloned.1.call-start = ((), (), s32[]{:S(2)}) async-start(), calls=%async_computation.17 | async-start | bytes 1536000 | tf_op jit(solution)/shard_map/reduce_scatter | solution.py:96
  54.4 88.3 %reduce-scatter.15.cloned.1.call-start = ((), (), s32[]{:S(2)}) async-start(), calls=%async_computation.21 | async-start | bytes 1536000 | tf_op jit(solution)/shard_map/reduce_scatter | solution.py:96
  86.9 88.8 %all-gather.9.cloned.1.call-start = ((), (), s32[]{:S(2)}) async-start(), calls=%async_computation.18 | async-start | bytes 5898240 | tf_op jit(solution)/shard_map/all_gather | solution.py:25
  87.5 118.9 %all-gather.11.cloned.1.call-start = ((), (), s32[]{:S(2)}) async-start(), calls=%async_computation.19 | async-start | bytes 5898240 | tf_op jit(solution)/shard_map/all_gather | solution.py:26
  88.1 177.3 %copy-start.116 = (pred[2,197]{1,0:T(4,128)(4,1)}, pred[2,197]{1,0:T(4,128)(4,1)S(1)}, u32[]{:S(2)}) copy-start(pred[2,197]{1,0:T(4,128)(4,1)S(1)} %get-tuple-element.119) | copy-start | bytes 1186
  88.1 196.9 %copy-start.117 = (pred[2,197]{1,0:T(4,128)(4,1)}, pred[2,197]{1,0:T(4,128)(4,1)S(1)}, u32[]{:S(2)}) copy-start(pred[2,197]{1,0:T(4,128)(4,1)S(1)} %get-tuple-element.118) | copy-start | bytes 1186
  147.7 23.5 %all-to-all-start = ((bf16[4,2,64,768]{3,2,1,0:T(8,128)(2,1)}), bf16[4,2,64,768]{3,2,1,0:T(8,128)(2,1)S(1)}, u32[]{:S(2)}, u32[]{:S(2)}) async-start(bf16[4,2,64,768]{3,2,1,0:T(8,128)(2,1)} %bitcast.19), calls=%async_computation.1 | async-start | bytes 1572864 | tf_op jit(solution)/shard_map/all_to_all | solution.py:118
  171.2 23.9 %all-to-all-start.2 = ((bf16[4,2,64,768]{3,2,1,0:T(8,128)(2,1)}), bf16[4,2,64,768]{3,2,1,0:T(8,128)(2,1)}, u32[]{:S(2)}, u32[]{:S(2)}) async-start(bf16[4,2,64,768]{3,2,1,0:T(8,128)(2,1)} %bitcast.50), calls=%async_computation.4 | async-start | bytes 1572864 | tf_op jit(solution)/shard_map/all_to_all | solution.py:118
  175.4 57.8 %all-reduce.8.cloned.1.call-start = ((), (), s32[]{:S(2)}) async-start(), calls=%async_computation.31 | async-start | bytes 3145728 | tf_op jit(solution)/shard_map/psum | solution.py:123
  235.3 25.4 %all-to-all-start.1 = ((bf16[4,2,64,768]{3,2,1,0:T(8,128)(2,1)}), bf16[4,2,64,768]{3,2,1,0:T(8,128)(2,1)S(1)}, u32[]{:S(2)}, u32[]{:S(2)}) async-start(bf16[4,2,64,768]{3,2,1,0:T(8,128)(2,1)} %copy.169), calls=%async_computation.2 | async-start | bytes 1572864 | tf_op jit(solution)/shard_map/all_to_all | solution.py:125
  243.1 164.7 %copy-start.91 = (f32[197]{0:T(256)}, f32[197]{0:T(256)S(1)}, u32[]{:S(2)}) copy-start(f32[197]{0:T(256)S(1)} %get-tuple-element.132) | copy-start | bytes 2368
  243.2 163.9 %copy-start.66 = (f32[197,8]{0,1:T(8,128)}, f32[197,8]{0,1:T(8,128)S(1)}, u32[]{:S(2)}) copy-start(f32[197,8]{0,1:T(8,128)S(1)} %get-tuple-element.131) | copy-start | bytes 18916
  243.3 163.8 %copy-start.93 = (f32[197]{0:T(256)}, f32[197]{0:T(256)S(1)}, u32[]{:S(2)}) copy-start(f32[197]{0:T(256)S(1)} %get-tuple-element.130) | copy-start | bytes 2368
  260.7 24.4 %all-to-all-start.3 = ((bf16[4,2,64,768]{3,2,1,0:T(8,128)(2,1)}), bf16[4,2,64,768]{3,2,1,0:T(8,128)(2,1)}, u32[]{:S(2)}, u32[]{:S(2)}) async-start(bf16[4,2,64,768]{3,2,1,0:T(8,128)(2,1)} %copy.175), calls=%async_computation.5 | async-start | bytes 1572864 | tf_op jit(solution)/shard_map/all_to_all | solution.py:125
  265.3 141.7 %copy-start.96 = (f32[197]{0:T(256)}, f32[197]{0:T(256)S(1)}, u32[]{:S(2)}) copy-start(f32[197]{0:T(256)S(1)} %fusion.210) | copy-start | bytes 2368
  265.4 141.7 %copy-start.108 = (f32[197]{0:T(256)}, f32[197]{0:T(256)S(1)}, u32[]{:S(2)}) copy-start(f32[197]{0:T(256)S(1)} %fusion.208) | copy-start | bytes 2368
  295.2 23.9 %all-to-all-start.6 = ((bf16[4,2,64,768]{3,2,1,0:T(8,128)(2,1)}), bf16[4,2,64,768]{3,2,1,0:T(8,128)(2,1)}, u32[]{:S(2)}, u32[]{:S(2)}) async-start(bf16[4,2,64,768]{3,2,1,0:T(8,128)(2,1)} %bitcast.676), calls=%async_computation.9 | async-start | bytes 1572864 | tf_op jit(solution)/shard_map/all_to_all | solution.py:138
  319.1 23.9 %all-to-all-start.4 = ((bf16[4,2,64,768]{3,2,1,0:T(8,128)(2,1)}), bf16[4,2,64,768]{3,2,1,0:T(8,128)(2,1)}, u32[]{:S(2)}, u32[]{:S(2)}) async-start(bf16[4,2,64,768]{3,2,1,0:T(8,128)(2,1)} %bitcast.675), calls=%async_computation.6 | async-start | bytes 1572864 | tf_op jit(solution)/shard_map/all_to_all | solution.py:138
  323.3 51.6 %all-reduce.6.cloned.1.call-start = ((), (), s32[]{:S(2)}) async-start(), calls=%async_computation.30 | async-start | bytes 3145728 | tf_op jit(solution)/shard_map/psum | solution.py:155
  377.0 25.7 %all-to-all-start.5 = ((bf16[4,2,64,768]{3,2,1,0:T(8,128)(2,1)}), bf16[4,2,64,768]{3,2,1,0:T(8,128)(2,1)}, u32[]{:S(2)}, u32[]{:S(2)}) async-start(bf16[4,2,64,768]{3,2,1,0:T(8,128)(2,1)} %copy.180), calls=%async_computation.7 | async-start | bytes 1572864 | tf_op jit(solution)/shard_map/all_to_all | solution.py:157
  402.6 24.0 %all-to-all-start.7 = ((bf16[4,2,64,768]{3,2,1,0:T(8,128)(2,1)}), bf16[4,2,64,768]{3,2,1,0:T(8,128)(2,1)}, u32[]{:S(2)}, u32[]{:S(2)}) async-start(bf16[4,2,64,768]{3,2,1,0:T(8,128)(2,1)} %copy.194), calls=%async_computation.10 | async-start | bytes 1572864 | tf_op jit(solution)/shard_map/all_to_all | solution.py:157
  406.8 74.6 %all-gather.17.cloned.1.call-start = ((), (), s32[]{:S(2)}) async-start(), calls=%async_computation.24 | async-start | bytes 1536000 | tf_op jit(solution)/shard_map/all_gather | solution.py:175
  451.1 62.8 %all-gather.15.cloned.1.call-start = ((), (), s32[]{:S(2)}) async-start(), calls=%async_computation.22 | async-start | bytes 1536000 | tf_op jit(solution)/shard_map/all_gather | solution.py:175
  453.2 108.1 %reduce-scatter.27.cloned.1.call-start = ((), (), s32[]{:S(2)}) async-start(), calls=%async_computation.29 | async-start | bytes 491520
  523.2 55.0 %reduce-scatter.25.cloned.1.call-start = ((), (), s32[]{:S(2)}) async-start(), calls=%async_computation.28 | async-start | bytes 1228800
  533.4 77.4 %reduce-scatter.17.cloned.1.call-start = ((), (), s32[]{:S(2)}) async-start(), calls=%async_computation.23 | async-start | bytes 1536000 | tf_op jit(solution)/shard_map/reduce_scatter | solution.py:206
  537.5 105.0 %reduce-scatter.19.cloned.1.call-start = ((), (), s32[]{:S(2)}) async-start(), calls=%async_computation.25 | async-start | bytes 1536000 | tf_op jit(solution)/shard_map/reduce_scatter | solution.py:206
  541.2 184.0 %reduce-scatter.21.cloned.1.call-start = ((), (), s32[]{:S(2)}) async-start(), calls=%async_computation.26 | async-start | bytes 5898240 | tf_op jit(solution)/shard_map/reduce_scatter | solution.py:219
  549.4 212.1 %reduce-scatter.23.cloned.1.call-start = ((), (), s32[]{:S(2)}) async-start(), calls=%async_computation.27 | async-start | bytes 5898240 | tf_op jit(solution)/shard_map/reduce_scatter | solution.py:222
  (135 other events, 2078.1 us)
Sparse Core Ops, SparseCore 0:
  12.9 33.8 all-gather.6
  48.9 30.2 all-gather.12
  82.1 29.4 reduce-scatter.12
  113.8 28.8 reduce-scatter.14
  213.7 19.4 all-reduce.7
  355.4 19.4 all-reduce.5
  451.2 30.1 all-gather.16
  483.6 30.2 all-gather.14
Sparse Core Ops, SparseCore 1:
  89.2 56.0 all-gather.8
  147.0 56.8 all-gather.10
  523.3 23.8 reduce-scatter.26
  550.7 27.4 reduce-scatter.24
  580.5 30.2 reduce-scatter.16
  613.7 28.8 reduce-scatter.18
  645.4 56.3 reduce-scatter.20
  704.6 56.8 reduce-scatter.22
where the time goes:
time: 782 us; the launch traced here: 772 us
  waiting for transfers between devices  391 us (50%)
  matrix products  120 us (15%)
  blocking collectives  103 us (13%)
  local copies, waits for them, and re-layouts  53.2 us (7%)
  other arithmetic  50.3 us (6%)
  starting transfers between devices  36.3 us (5%)
  between operations  18.2 us (2%)
    psum x1, blocking collectives, on_device(): lax.psum((grad_gain_one, grad_gain_two, grad_router), ('fsdp', 'head'))  76.4 us
    reduce_scatter x2, waiting for transfers between devices, on_device(): lax.psum_scatter(row_part.astype(jnp.bfloat16), 'head', scatter_dimension...  60.7 us
    all_gather x2, waiting for transfers between devices, on_device(): lax.all_gather(hidden_grad.astype(bf16), 'head', axis=0, tiled=True)  54.3 us
    reduce_scatter x2, waiting for transfers between devices, on_device(): lax.psum_scatter(partial_att.astype(jnp.bfloat16), 'head', scatter_dimens...  51.8 us
    all_to_all x2, waiting for transfers between devices, on_device(): lax.all_to_all(expert_out, 'head', split_axis=0, concat_axis=0, tiled=True)  33.9 us
    reduce_scatter x1, waiting for transfers between devices, on_device(): lax.psum_scatter(grad_down.astype(jnp.bfloat16), 'fsdp', scatter_dimensio...  33.3 us
    all_gather x2, waiting for transfers between devices, on_device(): rows_all = lax.all_gather(normed.astype(bf16), 'head', axis=0, tiled=True)  29.8 us
    all_to_all x2, waiting for transfers between devices, on_device(): lax.all_to_all(buffer, 'head', split_axis=0, concat_axis=0, tiled=True)  26.2 us
  transfers between devices with their start and end apart: 24, of which 20 were waited for; matrix products, arithmetic and copies ran while one was open for 18% of the time, Pallas kernels for 0%

commit v1 on v0

v1 whole, which is shorter than its diff:
```python
import jax
import jax.numpy as jnp
from jax import lax
from jax.sharding import PartitionSpec as P

HD = 64
TOP = 2
CAP = 64

highest = lax.Precision.HIGHEST
norm_eps = 1e-06
f32 = jnp.float32
bf16 = jnp.bfloat16


def norm_rows(values, gain_vec):
    centre = values - jnp.mean(values, axis=-1, keepdims=True)
    spread = jnp.mean(centre * centre, axis=-1, keepdims=True)
    return centre * lax.rsqrt(spread + norm_eps) * gain_vec


def gelu_exact(values):
    return jax.nn.gelu(values, approximate=False)


def softmax_last(values):
    return jax.nn.softmax(values, axis=-1)


def ein(spec, left, right):
    return jnp.einsum(spec, left, right, preferred_element_type=f32)


def swap(values):
    return lax.ppermute(values, "tensor", ((0, 1), (1, 0)))


def pick(values):
    return lax.dynamic_index_in_dim(values, lax.axis_index("tensor"), 0, keepdims=False)


def both(mine):
    other = swap(mine)
    first = lax.axis_index("tensor") == 0
    return jnp.stack([jnp.where(first, mine, other), jnp.where(first, other, mine)])


def on_device(
    activations,
    w_qkv,
    w_out,
    gain_one,
    gain_two,
    w_router,
    w_in,
    w_down,
    routes,
    slot_index,
    keep_mask,
    cotangent,
):
    _, img_count, seq_length, width = activations.shape
    groups = lax.axis_size("head")
    local_heads = w_qkv.shape[2] // HD
    local_experts = w_in.shape[0]
    total_experts = local_experts * groups
    slot_count = total_experts * CAP
    tok_rows = img_count * seq_length
    head_scale = HD ** (-0.5)

    qkv_full = lax.all_gather(w_qkv, "fsdp", axis=1, tiled=True)
    out_full = lax.all_gather(w_out, "fsdp", axis=1, tiled=True)

    inputs = pick(activations).astype(f32)
    upstream = pick(cotangent).astype(f32).reshape(tok_rows, width)
    route_rows = pick(routes).reshape(tok_rows, TOP)
    slot_rows = pick(slot_index).reshape(tok_rows, TOP)
    keep_int = pick(keep_mask).reshape(tok_rows, TOP)

    normed, norm_back_one = jax.vjp(norm_rows, inputs, gain_one)
    rows_all = lax.all_gather(normed.astype(bf16), "head", axis=0, tiled=True)
    in_full = lax.all_gather(w_in, "fsdp", axis=1, tiled=True)
    down_full = lax.all_gather(w_down, "fsdp", axis=2, tiled=True)
    image_total = rows_all.shape[0]
    head_shape = (image_total, seq_length, local_heads, HD)
    project = ein("bsd,pde->pbse", rows_all, qkv_full)
    queries = (project[0] * head_scale).astype(bf16).reshape(head_shape)
    key_rows = project[1].astype(bf16).reshape(head_shape)
    value_rows = project[2].astype(bf16).reshape(head_shape)
    scores = ein("bqhd,bkhd->bhqk", queries, key_rows)
    top_score = jnp.max(scores, axis=-1, keepdims=True)
    expo_scores = jnp.exp(scores - top_score)
    row_total = jnp.sum(expo_scores, axis=-1, keepdims=True)
    attn_full = expo_scores / row_total
    attn_low = attn_full.astype(bf16)
    mixed_heads = ein("bhqk,bkhd->bqhd", attn_low, value_rows)
    mixed_heads = mixed_heads.reshape(image_total, seq_length, local_heads * HD).astype(bf16)
    partial_att = ein("bsc,cd->bsd", mixed_heads, out_full)
    attended = lax.psum_scatter(
        partial_att.astype(bf16), "head", scatter_dimension=0, tiled=True
    ).astype(f32)
    hidden = inputs + attended
    normed_two, norm_back_two = jax.vjp(norm_rows, hidden, gain_two)
    token_low = normed_two.astype(bf16).reshape(tok_rows, width)
    logits = jnp.dot(token_low, w_router, preferred_element_type=f32)
    gate_probs, softmax_back = jax.vjp(softmax_last, logits)

    keep_rows = keep_int.astype(f32)
    expert_ids = jnp.arange(total_experts, dtype=jnp.int32)
    slot_ids = jnp.arange(slot_count, dtype=jnp.int32)
    chosen = (route_rows[:, :, None] == expert_ids[None, None, :]).astype(f32)
    gate_values = jnp.sum(gate_probs[:, None, :] * chosen, axis=2) * keep_rows
    flat_slot = route_rows * CAP + slot_rows
    onehot = (
        (flat_slot.T[:, :, None] == slot_ids[None, None, :]) & (keep_int.T[:, :, None] == 1)
    ).astype(bf16)
    weighted = (gate_values.T[:, :, None] * upstream[None, :, :]).astype(bf16)
    tokens_two = jnp.broadcast_to(token_low[None], weighted.shape)
    sent = ein("ktc,ktd->cd", onehot, jnp.concatenate([tokens_two, weighted], axis=-1))
    sent = sent.astype(bf16).reshape(groups, local_experts, CAP, 2 * width)
    mine = lax.all_to_all(sent, "head", split_axis=0, concat_axis=0, tiled=True)
    slots = jnp.stack([mine, swap(mine)])
    received = slots[..., :width]
    slot_grad = slots[..., width:]

    up_proj = ein("mgecd,edf->emgcf", received, in_full)
    active, gelu_back = jax.vjp(gelu_exact, up_proj)
    active = active.astype(bf16)
    partial_out = ein("emgcf,efd->mgecd", active, down_full)
    active_grad = ein("mgecd,efd->emgcf", slot_grad, down_full)
    up_grad = gelu_back(active_grad)[0].astype(bf16)
    partial_in = ein("emgcf,edf->mgecd", up_grad, in_full)
    grad_down = ein("emgcf,mgecd->efd", active, slot_grad)
    grad_in = ein("mgecd,emgcf->edf", received, up_grad)

    partial = jnp.concatenate([partial_out, partial_in], axis=-1)
    back = (partial[0] + swap(partial[1].astype(bf16)).astype(f32)).astype(bf16)
    back = lax.all_to_all(back, "head", split_axis=0, concat_axis=0, tiled=True)
    back = back.reshape(slot_count, 2 * width)
    picked_two = ein("ktc,cd->ktd", onehot, back)
    picked = picked_two[..., :width]
    token_grad = picked_two[0, :, width:] + picked_two[1, :, width:]
    moe_out = jnp.sum(gate_values.T[:, :, None] * picked, axis=0)
    block_out = (hidden + moe_out.reshape(img_count, seq_length, width)).astype(bf16)

    gate_grad = jnp.sum(upstream[None] * picked, axis=-1).T * keep_rows
    prob_grad = jnp.sum(gate_grad[:, :, None] * chosen, axis=1)
    logit_grad = softmax_back(prob_grad)[0]
    grad_router = jnp.dot(token_low.astype(f32).T, logit_grad, precision=highest)
    token_grad = token_grad + jnp.dot(logit_grad, w_router.astype(f32).T, precision=highest)
    hidden_part, grad_gain_two = norm_back_two(token_grad.reshape(img_count, seq_length, width))
    hidden_grad = upstream.reshape(img_count, seq_length, width) + hidden_part

    att_grad_all = lax.all_gather(hidden_grad.astype(bf16), "head", axis=0, tiled=True)
    grad_out = ein("bsc,bsd->cd", mixed_heads, att_grad_all)
    mixed_grad = ein("bsd,cd->bsc", att_grad_all, out_full).astype(bf16).reshape(head_shape)
    value_grad = ein("bhqk,bqhd->bkhd", attn_low, mixed_grad).astype(bf16)
    prob_grads = ein("bqhd,bkhd->bhqk", mixed_grad, value_rows)
    row_delta = jnp.sum(prob_grads * attn_full, axis=-1, keepdims=True)
    score_grad = (attn_full * (prob_grads - row_delta)).astype(bf16)
    query_grad = (ein("bhqk,bkhd->bqhd", score_grad, key_rows) * head_scale).astype(bf16)
    key_grad = ein("bhqk,bqhd->bkhd", score_grad, queries).astype(bf16)
    proj_grad = jnp.stack([query_grad, key_grad, value_grad]).reshape(
        3, image_total, seq_length, local_heads * HD
    )
    row_part = ein("pbse,pde->bsd", proj_grad, qkv_full)
    row_grad = lax.psum_scatter(
        row_part.astype(bf16), "head", scatter_dimension=0, tiled=True
    ).astype(f32)
    grad_qkv = ein("bsd,pbse->pde", rows_all, proj_grad)
    input_part, grad_gain_one = norm_back_one(row_grad)
    input_grad = hidden_grad + input_part

    def owner(part, dim):
        part = lax.psum_scatter(part.astype(bf16), "fsdp", scatter_dimension=dim, tiled=True)
        return part

    def owner_two(part, dim):
        part = owner(part, dim)
        return part.astype(f32) + swap(part).astype(f32)

    small = lax.psum((grad_gain_one, grad_gain_two, grad_router), ("fsdp", "head", "tensor"))
    return (
        both(block_out),
        both(input_grad),
        owner_two(grad_qkv, 1),
        owner_two(grad_out, 1),
        *small,
        owner(grad_in, 1).astype(f32),
        owner(grad_down, 2).astype(f32),
    )


def solution(mesh):
    rows = P(None, ("fsdp", "head"), None, None)
    in_specs = (
        rows,
        P(None, "fsdp", "head"),
        P("head", "fsdp"),
        P(),
        P(),
        P(),
        P("head", "fsdp", "tensor"),
        P("head", "tensor", "fsdp"),
        rows,
        rows,
        rows,
        rows,
    )
    out_specs = (
        rows,
        rows,
        P(None, "fsdp", "head"),
        P("head", "fsdp"),
        P(),
        P(),
        P(),
        P("head", "fsdp", "tensor"),
        P("head", "tensor", "fsdp"),
    )
    return jax.shard_map(
        on_device, mesh=mesh, in_specs=in_specs, out_specs=out_specs, check_vma=False
    )
```

time: 782 us -> 525 us (0.67)
  waiting for transfers between devices: 391 us -> 247 us
  matrix products: 120 us -> 65.6 us
  starting transfers between devices: 36.3 us -> 5.79 us
  local copies, waits for them, and re-layouts: 53.2 us -> 28.8 us
    all_to_all x8 -> x1, waiting for transfers between devices: 105 us -> 37.1 us  [on_device(): back = lax.all_to_all(back, 'head', split_axis=0, concat_axis=0, tiled=True)]
    dot_general x46 -> x20, matrix products: 119 us -> 63.2 us  [the longest x19 62.4 us: ein(): return jnp.einsum(spec, left, right, preferred_element_type=f32)]
    all_to_all x0 -> x1, blocking collectives: none -> 39.4 us  [on_device(): mine = lax.all_to_all(sent, 'head', split_axis=0, concat_axis=0, tiled=True)]
    psum x2 -> x0, waiting for transfers between devices: 39.3 us -> none  [the longest x1 19.6 us: on_device(): lax.psum(partial_out.astype(jnp.bfloat16), 'tensor').astype(jnp.float32)]
    psum x1, blocking collectives: 76.4 us -> 40.7 us  [on_device(): lax.psum((grad_gain_one, grad_gain_two, grad_router), ('fsdp', 'head', 't...]
    all_to_all x8 -> x1, starting transfers between devices: 34.8 us -> 4.59 us  [on_device(): back = lax.all_to_all(back, 'head', split_axis=0, concat_axis=0, tiled=True)]
    all_gather x2 -> x1, waiting for transfers between devices: 29.8 us -> 3.05 us  [on_device(): rows_all = lax.all_gather(normed.astype(bf16), 'head', axis=0, tiled=True)]
    all_gather x2 -> x1, waiting for transfers between devices: 54.3 us -> 29.3 us  [on_device(): lax.all_gather(hidden_grad.astype(bf16), 'head', axis=0, tiled=True)]
  transfers between devices with their start and end apart: 24 -> 17, of which waited for: 20 -> 13; matrix products, arithmetic and copies ran while one was open for 18% -> 15% of each run, Pallas kernels for 0% -> 0%
where the time goes in v1:
time: 525 us; the launch traced here: 518 us
  waiting for transfers between devices  247 us (47%)
  blocking collectives  110 us (21%)
  matrix products  65.6 us (12%)
  other arithmetic  44.1 us (8%)
  local copies, waits for them, and re-layouts  28.8 us (5%)
  between operations  16.4 us (3%)
  starting transfers between devices  5.79 us (1%)
    reduce_scatter x2, waiting for transfers between devices, owner(): lax.psum_scatter(part.astype(bf16), 'fsdp', scatter_dimension=dim, tiled=...  69.7 us
    dot_general x19, matrix products, ein(): return jnp.einsum(spec, left, right, preferred_element_type=f32)  62.4 us
    psum x1, blocking collectives, on_device(): lax.psum((grad_gain_one, grad_gain_two, grad_router), ('fsdp', 'head', 't...  40.7 us
    all_to_all x1, blocking collectives, on_device(): mine = lax.all_to_all(sent, 'head', split_axis=0, concat_axis=0, tiled=True)  39.4 us
    all_to_all x1, waiting for transfers between devices, on_device(): back = lax.all_to_all(back, 'head', split_axis=0, concat_axis=0, tiled=True)  37.1 us
    all_gather x1, waiting for transfers between devices, on_device(): lax.all_gather(hidden_grad.astype(bf16), 'head', axis=0, tiled=True)  29.3 us
    reduce_scatter x1, waiting for transfers between devices, on_device(): lax.psum_scatter(row_part.astype(bf16), 'head', scatter_dimension=0, tile...  26.3 us
    reduce_scatter x1, waiting for transfers between devices, on_device(): lax.psum_scatter(partial_att.astype(bf16), 'head', scatter_dimension=0, t...  25.5 us
  transfers between devices with their start and end apart: 17, of which 13 were waited for; matrix products, arithmetic and copies ran while one was open for 15% of the time, Pallas kernels for 0%

profile of v1, /device:TPU:0, one launch (start us, length us, event | category | flops | bytes accessed | tf_op | source)
XLA Modules:
  0.0 517.9 jit_solution(9751888236601514068)
XLA Ops:
  12.1 19.2 %all_gather.19 = bf16[3,768,192]{2,0,1:T(4,128)(2,1)S(1)} all-gather(bf16[3,192,192]{2,0,1:T(4,128)(2,1)S(1)} %copy.105), channel_id=1, replica_groups=mesh['fsdp'=4,'head'=4,'tensor'=2] {'fsdp'}, dimensions={1}, use_global_device_ids=true | all-gather | bytes 1105920 | tf_op jit(solution)/shard_map/all_gather | solution.py:71
  32.3 10.4 %all_gather.20 = bf16[192,768]{0,1:T(8,128)(2,1)} all-gather(bf16[192,192]{0,1:T(8,128)(2,1)S(1)} %copy.108), channel_id=1, replica_groups=mesh['fsdp'=4,'head'=4,'tensor'=2] {'fsdp'}, dimensions={1}, use_global_device_ids=true | all-gather | bytes 368640 | tf_op jit(solution)/shard_map/all_gather | solution.py:72
  42.7 3.0 all-gather.5.cloned.1.call-done
  45.7 2.4 fusion.96
  59.4 25.5 %reduce-scatter.11.cloned.1.call-done = bf16[1,197,768]{2,1,0:T(8,128)(2,1)} async-done(((bf16[4,197,768]{2,1,0:T(8,128)(2,1)}), bf16[1,197,768]{2,1,0:T(8,128)(2,1)}) %reduce-scatter.11.cloned.1.call-update) | async-done | bytes 302608 | tf_op jit(solution)/shard_map/reduce_scatter | solution.py:99
  91.2 39.4 %all_to_all.10 = bf16[4,2,64,1536]{3,2,1,0:T(8,128)(2,1)S(1)} all-to-all(bf16[4,2,64,1536]{3,2,1,0:T(8,128)(2,1)S(1)} %bitcast.259), channel_id=1, replica_groups=mesh['fsdp'=4,'head'=4,'tensor'=2] {'head'}, dimensions={0} | all-to-all | bytes 3145728 | tf_op jit(solution)/shard_map/all_to_all | solution.py:121
  131.9 3.7 collective-permute-done
  135.7 3.9 pad_maximum_fusion.1
  139.6 7.0 %fusion.33 = (u8[2,2,64,1536]{3,2,1,0:T(8,128)(4,1)S(1)}, u8[2,2,64,1536]{3,2,1,0:T(8,128)(4,1)S(1)}, f32[2,2,4,64,1536]{4,3,2,1,0:T(8,128)S(1)}) fusion(bf16[2,4,2,64,768]{4,3,1,0,2:T(8,128)(2,1)} %get-tuple-element.63, bf16[2,768,1536]{2,1,0:T(8,128)(2,1)} %all-gather.7.cloned.1.call-done), kind=kOutput, calls=%fused_computation.59 | convolution fusion | flops 2435579904 | bytes 13369344 | tf_op jit(solution)/shard_map/mgecd,edf->emgcf/dot_general | solution.py:31
  146.6 2.6 copy-done.8
  149.2 15.2 %multiply_convert_fusion = (bf16[2,2,4,64,1536]{4,3,2,1,0:T(8,128)(2,1)}, f32[2,2,4,64,1536]{4,3,2,1,0:T(8,128)}) fusion(f32[2,2,4,64,1536]{4,3,2,1,0:T(8,128)S(1)} %get-tuple-element.79, u8[2,2,64,1536]{3,2,1,0:T(8,128)(4,1)S(1)} %get-tuple-element.46, u8[2,2,64,1536]{3,2,1,0:T(8,128)(4,1)S(1)} %get-tuple-element.45), kind=kLoop, calls=%fused_computation.13 | loop fusion | flops 110100480 | bytes 16515072 | tf_op jit(solution)/shard_map/convert_element_type | solution.py:128
  164.4 23.6 %all-gather.9.cloned.1.call-done = bf16[2,1536,768]{1,2,0:T(8,128)(2,1)} async-done(((bf16[2,1536,192]{1,2,0:T(8,128)(2,1)}), bf16[2,1536,768]{1,2,0:T(8,128)(2,1)}) %all-gather.9.cloned.1.call-update) | async-done | bytes 4718608 | tf_op jit(solution)/shard_map/all_gather | solution.py:83
  188.0 10.4 %add_convert_fusion = bf16[2,2,4,64,1536]{4,3,2,1,0:T(8,128)(2,1)S(1)} fusion(f32[2,2,4,64,1536]{4,3,2,1,0:T(8,128)} %get-tuple-element.59, bf16[2,4,2,64,768]{4,3,1,0,2:T(8,128)(2,1)} %get-tuple-element.62, f32[2,2,4,64,1536]{4,3,2,1,0:T(8,128)} %copy-done.8, bf16[2,1536,768]{1,2,0:T(8,128)(2,1)} %all-gather.9.cloned.1.call-done), kind=kOutput, calls=%fused_computation.12 | convolution fusion | flops 2437939200 | bytes 22020096 | tf_op jit(solution)/shard_map/mgecd,efd->emgcf/dot_general | solution.py:31
  198.4 5.7 %fusion.25 = f32[2,4,2,64,768]{4,3,1,0,2:T(8,128)S(1)} fusion(bf16[2,2,4,64,1536]{4,3,2,1,0:T(8,128)(2,1)S(1)} %add_convert_fusion, bf16[2,768,1536]{2,1,0:T(8,128)(2,1)} %all-gather.7.cloned.1.call-done), kind=kOutput, calls=%fused_computation.50 | convolution fusion | flops 2415919104 | bytes 11010048 | tf_op jit(solution)/shard_map/emgcf,edf->mgecd/dot_general | solution.py:31
  204.2 2.6 fusion.22
  207.1 3.4 collective-permute-done.1
  212.2 4.6 all-to-all-start.1
  217.0 37.1 %all-to-all-done.1 = bf16[4,2,64,1536]{3,2,1,0:T(8,128)(2,1)} async-done(((bf16[4,2,64,1536]{3,2,1,0:T(8,128)(2,1)}), bf16[4,2,64,1536]{3,2,1,0:T(8,128)(2,1)}, u32[]{:S(2)}, u32[]{:S(2)}) %all-to-all-start.1) | async-done | bytes 1572896 | tf_op jit(solution)/shard_map/all_to_all | solution.py:138
  254.1 2.3 fusion.46
  261.6 29.3 %all-gather.11.cloned.1.call-done = bf16[4,197,768]{2,1,0:T(8,128)(2,1)} async-done(((bf16[1,197,768]{2,1,0:T(8,128)(2,1)}), bf16[4,197,768]{2,1,0:T(8,128)(2,1)}) %all-gather.11.cloned.1.call-update) | async-done | bytes 1210384 | tf_op jit(solution)/shard_map/all_gather | solution.py:154
  303.0 3.5 bitcast_convert_fusion.2
  306.6 2.8 fusion.34
  312.7 7.2 %bitcast_convert_fusion.1 = bf16[2,768,1536]{2,1,0:T(8,128)(2,1)} fusion(bf16[2,2,4,64,1536]{4,3,2,1,0:T(8,128)(2,1)} %copy-done.35, bf16[2,4,2,64,768]{4,3,1,0,2:T(8,128)(2,1)} %get-tuple-element.63), kind=kOutput, calls=%fused_computation.3 | convolution fusion | flops 2418278400 | bytes 9437184 | tf_op jit(solution)/shard_map/mgecd,emgcf->edf/dot_general | solution.py:31
  321.3 6.3 %bitcast_convert_fusion = bf16[2,1536,768]{1,2,0:T(8,128)(2,1)} fusion(bf16[2,2,4,64,1536]{4,3,2,1,0:T(8,128)(2,1)} %get-tuple-element.58, bf16[2,4,2,64,768]{4,3,1,0,2:T(8,128)(2,1)S(1)} %copy-done.19), kind=kOutput, calls=%fused_computation.2 | convolution fusion | flops 2418278400 | bytes 9437184 | tf_op jit(solution)/shard_map/emgcf,mgecd->efd/dot_general | solution.py:31
  331.5 26.3 %reduce-scatter.13.cloned.1.call-done = bf16[1,197,768]{2,1,0:T(8,128)(2,1)} async-done(((bf16[4,197,768]{2,1,0:T(8,128)(2,1)}), bf16[1,197,768]{2,1,0:T(8,128)(2,1)}) %reduce-scatter.13.cloned.1.call-update) | async-done | bytes 302608 | tf_op jit(solution)/shard_map/reduce_scatter | solution.py:167
  364.5 22.8 %reduce-scatter.19.cloned.1.call-done = bf16[192,576]{1,0:T(8,128)(2,1)} async-done(((bf16[768,576]{1,0:T(8,128)(2,1)}), bf16[192,576]{1,0:T(8,128)(2,1)}) %reduce-scatter.19.cloned.1.call-update) | async-done | bytes 221200
  391.4 40.7 %all-reduce = (f32[768]{0:T(1024)}, f32[768]{0:T(1024)}, f32[768,8]{0,1:T(8,128)}) all-reduce(f32[768]{0:T(1024)S(1)} %get-tuple-element.51, f32[768]{0:T(1024)S(1)} %get-tuple-element.49, f32[768,8]{0,1:T(8,128)S(1)} %fusion.91), channel_id=1, replica_groups=mesh['fsdp'=4,'head'=4,'tensor'=2] {'fsdp','head','tensor'}, use_global_device_ids=true, to_apply=%region_23.24 | all-reduce | flops 7680 | bytes 61440 | tf_op jit(solution)/shard_map/psum | solution.py:182
  432.4 2.3 copy.131
  434.6 13.0 %reduce-scatter.15.cloned.1.call-done = bf16[2,192,1536]{2,1,0:T(8,128)(2,1)} async-done(((bf16[2,768,1536]{2,1,0:T(8,128)(2,1)}), bf16[2,192,1536]{2,1,0:T(8,128)(2,1)}) %reduce-scatter.15.cloned.1.call-update) | async-done | bytes 1179664 | tf_op jit(solution)/shard_map/reduce_scatter | solution.py:175
  447.6 3.0 convert_element_type.251
  450.6 56.8 %reduce-scatter.17.cloned.1.call-done = bf16[2,1536,192]{1,2,0:T(8,128)(2,1)} async-done(((bf16[2,1536,768]{1,2,0:T(8,128)(2,1)}), bf16[2,1536,192]{1,2,0:T(8,128)(2,1)}) %reduce-scatter.17.cloned.1.call-update) | async-done | bytes 1179664 | tf_op jit(solution)/shard_map/reduce_scatter | solution.py:175
  507.4 3.0 convert_element_type.253
  (178 shorter events, 62.5 us)
Async XLA Ops:
  8.0 37.7 %all-gather.5.cloned.1.call-start = ((), (), s32[]{:S(2)}) async-start(), calls=%async_computation.8 | async-start | bytes 1536000 | tf_op jit(solution)/shard_map/all_gather | solution.py:81
  9.9 22.3 %copy-start.27 = (bf16[192,192]{1,0:T(8,128)(2,1)S(1)}, bf16[192,192]{1,0:T(8,128)(2,1)}, u32[]{:S(2)}) copy-start(bf16[192,192]{1,0:T(8,128)(2,1)} %param.14) | copy-start | bytes 221188
  11.7 73.2 %reduce-scatter.11.cloned.1.call-start = ((), (), s32[]{:S(2)}) async-start(), calls=%async_computation.9 | async-start | bytes 1536000 | tf_op jit(solution)/shard_map/reduce_scatter | solution.py:99
  31.3 16.9 %copy-start.6 = (bf16[3,768,192]{2,0,1:T(4,128)(2,1)}, bf16[3,768,192]{2,0,1:T(4,128)(2,1)S(1)}, u32[]{:S(2)}) copy-start(bf16[3,768,192]{2,0,1:T(4,128)(2,1)S(1)} %all_gather.19) | copy-start | bytes 2654212
  51.2 243.2 %copy-start.2 = (f32[4,3,197,197]{2,3,1,0:T(8,128)}, f32[4,3,197,197]{2,3,1,0:T(8,128)S(1)}, u32[]{:S(2)}) copy-start(f32[4,3,197,197]{2,3,1,0:T(8,128)S(1)} %get-tuple-element.76) | copy-start | bytes 5588500
  55.3 32.0 %copy-start.29 = (f32[768]{0:T(1024)S(1)}, f32[768]{0:T(1024)}, u32[]{:S(2)}) copy-start(f32[768]{0:T(1024)} %param.16) | copy-start | bytes 9220
  55.3 33.1 %copy-start.30 = (bf16[768,8]{0,1:T(8,128)(2,1)S(1)}, bf16[768,8]{0,1:T(8,128)(2,1)}, u32[]{:S(2)}) copy-start(bf16[768,8]{0,1:T(8,128)(2,1)} %param.17) | copy-start | bytes 36868
  55.3 84.3 %all-gather.7.cloned.1.call-start = ((), (), s32[]{:S(2)}) async-start(), calls=%async_computation.10 | async-start | bytes 5898240 | tf_op jit(solution)/shard_map/all_gather | solution.py:82
  55.9 132.1 %all-gather.9.cloned.1.call-start = ((), (), s32[]{:S(2)}) async-start(), calls=%async_computation.11 | async-start | bytes 5898240 | tf_op jit(solution)/shard_map/all_gather | solution.py:83
  131.9 3.8 collective-permute-start
  198.4 5.7 %copy-start.35 = (bf16[2,2,4,64,1536]{4,3,2,1,0:T(8,128)(2,1)}, bf16[2,2,4,64,1536]{4,3,2,1,0:T(8,128)(2,1)S(1)}, u32[]{:S(2)}) copy-start(bf16[2,2,4,64,1536]{4,3,2,1,0:T(8,128)(2,1)S(1)} %add_convert_fusion) | copy-start | bytes 9437188
  198.4 5.7 %copy-start.18 = (bf16[2,2,4,64,1536]{4,3,2,1,0:T(8,128)(2,1)S(1)}, bf16[2,2,4,64,1536]{4,3,2,1,0:T(8,128)(2,1)}, u32[]{:S(2)}) copy-start(bf16[2,2,4,64,1536]{4,3,2,1,0:T(8,128)(2,1)} %get-tuple-element.58) | copy-start | bytes 9437188
  198.4 5.8 %copy-start.34 = (bf16[2,1536,768]{1,2,0:T(8,128)(2,1)S(1)}, bf16[2,1536,768]{1,2,0:T(8,128)(2,1)}, u32[]{:S(2)}) copy-start(bf16[2,1536,768]{1,2,0:T(8,128)(2,1)} %all-gather.9.cloned.1.call-done) | copy-start | bytes 14155780
  207.1 3.5 collective-permute-start.1
  212.2 42.0 %all-to-all-start.1 = ((bf16[4,2,64,1536]{3,2,1,0:T(8,128)(2,1)}), bf16[4,2,64,1536]{3,2,1,0:T(8,128)(2,1)}, u32[]{:S(2)}, u32[]{:S(2)}) async-start(bf16[4,2,64,1536]{3,2,1,0:T(8,128)(2,1)} %copy.114), calls=%async_computation.2 | async-start | bytes 3145728 | tf_op jit(solution)/shard_map/all_to_all | solution.py:138
  216.8 74.2 %all-gather.11.cloned.1.call-start = ((), (), s32[]{:S(2)}) async-start(), calls=%async_computation.12 | async-start | bytes 1536000 | tf_op jit(solution)/shard_map/all_gather | solution.py:154
  256.4 4.3 copy-start.4
  258.1 32.9 %copy-start.17 = (bf16[192,768]{0,1:T(8,128)(2,1)S(1)}, bf16[192,768]{0,1:T(8,128)(2,1)}, u32[]{:S(2)}) copy-start(bf16[192,768]{0,1:T(8,128)(2,1)} %all_gather.20) | copy-start | bytes 884740
  261.6 68.7 %reduce-scatter.21.cloned.1.call-start = ((), (), s32[]{:S(2)}) async-start(), calls=%async_computation.17 | async-start | bytes 491520
  298.0 5.0 copy-start.7
  300.6 57.1 %reduce-scatter.13.cloned.1.call-start = ((), (), s32[]{:S(2)}) async-start(), calls=%async_computation.13 | async-start | bytes 1536000 | tf_op jit(solution)/shard_map/reduce_scatter | solution.py:167
  306.5 80.7 %reduce-scatter.19.cloned.1.call-start = ((), (), s32[]{:S(2)}) async-start(), calls=%async_computation.16 | async-start | bytes 1228800
  312.7 134.9 %reduce-scatter.15.cloned.1.call-start = ((), (), s32[]{:S(2)}) async-start(), calls=%async_computation.14 | async-start | bytes 5898240 | tf_op jit(solution)/shard_map/reduce_scatter | solution.py:175
  319.9 187.4 %reduce-scatter.17.cloned.1.call-start = ((), (), s32[]{:S(2)}) async-start(), calls=%async_computation.15 | async-start | bytes 5898240 | tf_op jit(solution)/shard_map/reduce_scatter | solution.py:175
  327.6 30.2 %copy-start.28 = (f32[768]{0:T(1024)S(1)}, f32[768]{0:T(1024)}, u32[]{:S(2)}) copy-start(f32[768]{0:T(1024)} %param.15) | copy-start | bytes 9220
  327.6 32.8 %copy-start.5 = (bf16[1,1,197,768]{3,0,2,1:T(2,128)(2,1)S(1)}, bf16[1,1,197,768]{3,0,2,1:T(2,128)(2,1)}, u32[]{:S(2)}) copy-start(bf16[1,1,197,768]{3,0,2,1:T(2,128)(2,1)} %copy-done.3) | copy-start | bytes 907780
  327.6 32.8 %copy-start.10 = (f32[1,197,768]{2,1,0:T(8,128)S(1)}, f32[1,197,768]{2,1,0:T(8,128)}, u32[]{:S(2)}) copy-start(f32[1,197,768]{2,1,0:T(8,128)} %copy-done.9) | copy-start | bytes 1815556
  328.6 1.6 collective-permute-start.2
  331.3 57.5 %collective-permute-start.5 = (bf16[192,192]{1,0:T(8,128)(2,1)S(1)}, bf16[192,192]{1,0:T(8,128)(2,1)S(1)}, u32[]{:S(2)}, u32[]{:S(2)}) collective-permute-start(bf16[192,192]{1,0:T(8,128)(2,1)S(1)} %copy.150), channel_id=1, source_target_pairs={{0,1},{1,0},{2,3},{3,2},{4,5},{5,4},{6,7},{7,6},{8,9},{9,8},{10,11... | collective-permute-start | bytes 221192 | tf_op jit(solution)/shard_map/ppermute | solution.py:35
  363.1 69.0 %collective-permute-start.3 = (f32[1,197,768]{2,0,1:T(1,128)}, f32[1,197,768]{2,0,1:T(1,128)S(1)}, u32[]{:S(2)}, u32[]{:S(2)}) collective-permute-start(f32[1,197,768]{2,0,1:T(1,128)} %copy.123), channel_id=1, source_target_pairs={{0,1},{1,0},{2,3},{3,2},{4,5},{5,4},{6,7},{7,6},{8,9},{9,8},{10,11... | collective-permute-start | bytes 1815560 | tf_op jit(solution)/shard_map/ppermute | solution.py:35
  388.6 1.6 collective-permute-start.4
  432.4 78.0 %copy-start.1 = (bf16[2,1,197,768]{3,0,2,1:T(2,128)(2,1)S(1)}, bf16[2,1,197,768]{3,0,2,1:T(2,128)(2,1)}, u32[]{:S(2)}) copy-start(bf16[2,1,197,768]{3,0,2,1:T(2,128)(2,1)} %param.12) | copy-start | bytes 1815556
  (21 other events, 47.6 us)
Sparse Core Ops, SparseCore 0:
  11.9 33.8 all-gather.4
  55.4 29.4 reduce-scatter.10
  261.7 29.2 all-gather.10
Sparse Core Ops, SparseCore 1:
  57.7 56.0 all-gather.6
  132.0 55.9 all-gather.8
  300.7 23.8 reduce-scatter.20
  327.5 30.2 reduce-scatter.12
  361.3 25.9 reduce-scatter.18
  390.3 57.3 reduce-scatter.14
  450.5 56.8 reduce-scatter.16
